TPU v7x, 32 devices: a whole 2x2x4 slice. The times are simulated.
32 devices in a mesh: wide: 8 (over y, x, core), narrow: 4 (over z).
Axes of the slice: x: 2, y: 2, z: 4, core: 2. Of those that a mesh axis runs over, the one named last changes fastest.
Arguments:
- measures: float32 [2, 48, 262144], P(None, 'narrow', 'wide'), may hold values from 0.1 to 10
- sku_brand: int32 [262144], P('wide'), may hold values from 0 to 8191, as said below
- sku_count: int32 [8], P('wide'), may hold values from 1024 to 32768, as said below
- brand_slot: int32 [8192], replicated, may hold values from 0 to 8191, as said below
- brand_category: int32 [8192], replicated, may hold values from 0 to 499
Outputs:
- brand_index: float32 [2, 48, 8192], P(None, 'narrow', 'wide')
- category_index: float32 [2, 48, 500], P(None, 'narrow')
Inputs may be any that keep to these rules, and one draw needn't show every extreme that they name: `sku_count`: the largest count is 32768 in every draw; the others are skewed below it. brand_slot is a permutation; columns k * 1024 to (k + 1) * 1024 - 1 form the k-th owner block. `sku_brand`: in every tile, slots o * 128 to (o + 1) * 128 - 1 name 128 distinct brands whose columns lie in owner block o, for every owner block o; every later slot of the tile names one of these brands; every brand is named by some live SKU.
All inputs are finite; a program needn't handle non-finite values.
Results may differ from a plain program's by a relative error of at most 0.002.
Values sent between devices are 32-bit elements; how exact they have to be, the bound alone decides.
A program may use at most 64 MiB of HBM per device.

v0:
```python
import math
import jax
import jax.numpy as jnp
from jax import lax
from jax.sharding import PartitionSpec as P

WEEKS = 48
CATS = 500
CAP = 128


def body(measures, sku_brand, sku_count, brand_slot, brand_category):
    kinds_here, weeks_local, tile_size = measures.shape
    measure_rows = kinds_here * weeks_local
    flat = measures.reshape(measure_rows, tile_size)
    wide_size = lax.axis_size("wide")
    brand_total = brand_slot.shape[0]
    owned_width = brand_total // wide_size
    list_count = wide_size * CAP
    live_count = sku_count[0]
    list_brands = sku_brand[:list_count]
    own_index = lax.axis_index("wide")
    own_columns = own_index * owned_width + jnp.arange(owned_width, dtype=jnp.int32)
    category_ids = jnp.arange(CATS, dtype=jnp.int32)
    brand_block = math.gcd(1024, brand_total)
    brand_trips = brand_total // brand_block

    def lookup(block_index, carry):
        list_columns, my_category, category_size = carry
        offset = block_index * brand_block
        block_slots = lax.dynamic_slice_in_dim(brand_slot, offset, brand_block, 0)
        block_cats = lax.dynamic_slice_in_dim(brand_category, offset, brand_block, 0)
        block_ids = offset + jnp.arange(brand_block, dtype=jnp.int32)
        list_columns = list_columns + jnp.sum(
            jnp.where(list_brands[:, None] == block_ids[None, :], block_slots[None, :], 0), axis=1
        )
        my_category = my_category + jnp.sum(
            jnp.where(own_columns[:, None] == block_slots[None, :], block_cats[None, :], 0), axis=1
        )
        category_size = category_size + jnp.sum(
            (block_cats[:, None] == category_ids[None, :]).astype(jnp.float32), axis=0
        )
        return (list_columns, my_category, category_size)

    start_lookup = (
        jnp.zeros((list_count,), jnp.int32),
        jnp.zeros((owned_width,), jnp.int32),
        jnp.zeros((CATS,), jnp.float32),
    )
    list_columns, my_category, category_size = lax.fori_loop(0, brand_trips, lookup, start_lookup)
    high_part = flat.astype(jnp.bfloat16)
    first_rest = flat - high_part.astype(jnp.float32)
    middle_part = first_rest.astype(jnp.bfloat16)
    low_part = (first_rest - middle_part.astype(jnp.float32)).astype(jnp.bfloat16)
    stacked = jnp.concatenate([high_part, middle_part, low_part], axis=0)
    block_size = math.gcd(2048, tile_size)
    block_trips = (live_count + block_size - 1) // block_size

    def accumulate(block_index, totals):
        offset = block_index * block_size
        values = lax.dynamic_slice_in_dim(stacked, offset, block_size, 1)
        target = lax.dynamic_slice_in_dim(sku_brand, offset, block_size, 0)
        is_live = offset + jnp.arange(block_size, dtype=jnp.int32) < live_count
        values = jnp.where(is_live[None, :], values, jnp.zeros((), jnp.bfloat16))
        member_table = (target[:, None] == list_brands[None, :]).astype(jnp.bfloat16)
        return totals + jnp.dot(values, member_table, preferred_element_type=jnp.float32)

    start_sums = jnp.zeros((3 * measure_rows, list_count), jnp.float32)
    summed = lax.fori_loop(0, block_trips, accumulate, start_sums)
    compact = (
        summed[:measure_rows] + summed[measure_rows : 2 * measure_rows] + summed[2 * measure_rows :]
    )
    local_labels = (list_columns % owned_width).reshape(wide_size, CAP)
    packed = compact.reshape(measure_rows, wide_size, CAP).transpose(1, 0, 2)
    labels = local_labels.astype(jnp.float32)
    arrived, arrived_ids = (
        lax.all_to_all(packed, "wide", split_axis=0, concat_axis=0, tiled=True),
        lax.all_to_all(labels, "wide", split_axis=0, concat_axis=0, tiled=True),
    )
    flat_ids = arrived_ids.reshape(-1).astype(jnp.int32)
    flat_values = arrived.transpose(1, 0, 2).reshape(measure_rows, -1)
    placing = (flat_ids[:, None] == jnp.arange(owned_width, dtype=jnp.int32)[None, :]).astype(
        jnp.float32
    )
    owned_sums = jnp.dot(
        flat_values, placing, precision=lax.Precision.HIGHEST, preferred_element_type=jnp.float32
    )
    membership = (my_category[:, None] == category_ids[None, :]).astype(jnp.float32)
    category_part = jnp.dot(
        owned_sums, membership, precision=lax.Precision.HIGHEST, preferred_element_type=jnp.float32
    )
    category_sums = lax.psum(category_part, "wide")
    brand_category_sum = jnp.dot(
        category_sums,
        membership.T,
        precision=lax.Precision.HIGHEST,
        preferred_element_type=jnp.float32,
    )
    brand_peers = jnp.dot(
        membership,
        category_size,
        precision=lax.Precision.HIGHEST,
        preferred_element_type=jnp.float32,
    )
    brand_index = owned_sums * brand_peers[None, :] / brand_category_sum
    by_kind = category_sums.reshape(kinds_here, weeks_local, CATS)
    kind_totals = jnp.sum(by_kind, axis=(1, 2))
    grand_sum = lax.psum(kind_totals, "narrow") / WEEKS
    category_index = by_kind * CATS / grand_sum[:, None, None]
    return (brand_index.reshape(kinds_here, weeks_local, owned_width), category_index)


def solution(mesh):
    placed = (P(None, "narrow", "wide"), P("wide"), P("wide"), P(), P())
    return jax.shard_map(
        body,
        mesh=mesh,
        in_specs=placed,
        out_specs=(P(None, "narrow", "wide"), P(None, "narrow", None)),
        check_vma=False,
    )
```

profile of v0, /device:TPU:0, one launch (start us, length us, event | category | flops | bytes accessed | tf_op | source)
XLA Modules:
  0.0 159.0 jit_solution(1127724570599743675)
XLA Ops:
  1.4 23.3 %while.29 = (s32[]{:T(128)}, s32[1024]{0:T(1024)S(1)}, s32[1024]{0:T(1024)S(1)}, f32[500]{0:T(512)S(1)}, s32[1024]{0:T(1024)S(1)}, /*index=5*/s32[8192]{0:T(1024...) while((s32[]{:T(128)}, s32[1024]{0:T(1024)S(1)}, ...), condition=%wide.region_6.7_spmd.clone, body=%wide.region_2.6_spmd.clone.sunk | while | flops 7832059 | bytes 90110 | solution.py:50
  2.7 1.2 select_reduce_fusion.3
  5.7 1.2 select_reduce_fusion.3
  17.3 1.2 select_reduce_fusion.3
  20.2 1.2 select_reduce_fusion.3
  25.3 5.2 %all-to-all-start.1 = ((f32[8,1,128]{2,1,0:T(1,128)}), f32[8,1,128]{2,1,0:T(1,128)S(1)}, u32[]{:S(2)}, u32[]{:S(2)}) async-start(f32[8,1,128]{2,1,0:T(1,128)} %bitcast.3), calls=%async_computation.1 | async-start | bytes 8192 | tf_op jit(solution)/shard_map/all_to_all | solution.py:78
  31.1 5.6 %copy.21 = f32[2,12,32768]{2,1,0:T(8,128)} copy(f32[2,12,32768]{2,0,1:T(2,128)} %param.9) | data formatting | bytes 6291456 | tf_op args[0]
  36.8 2.6 %reshape.62 = f32[24,32768]{1,0:T(8,128)S(1)} reshape(f32[2,12,32768]{2,1,0:T(8,128)} %copy.21) | data formatting | bytes 6291456 | tf_op jit(solution)/shard_map/reshape | solution.py:15
  39.3 2.5 %fusion.31 = (bf16[24,32768]{1,0:T(8,128)(2,1)}, bf16[24,32768]{1,0:T(8,128)(2,1)}, bf16[24,32768]{1,0:T(8,128)(2,1)}) fusion(f32[24,32768]{1,0:T(8,128)S(1)} %reshape.62), kind=kLoop, calls=%fused_computation.49 | loop fusion | flops 5505024 | bytes 7864320 | tf_op jit(solution)/shard_map/convert_element_type | solution.py:51
  41.8 3.9 %pad_maximum_fusion = bf16[72,32768]{1,0:T(8,128)(2,1)} fusion(bf16[24,32768]{1,0:T(8,128)(2,1)} %get-tuple-element.277, bf16[24,32768]{1,0:T(8,128)(2,1)} %get-tuple-element.278, bf16[24,32768]{1,0:T(8,128)(2,1)} %get-tuple-element.276), kind=kLoop, calls=%fused_computation.23 | loop fusion | flops 14155776 | bytes 9437184 | tf_op jit(solution)/shard_map/concatenate | solution.py:55
  45.7 32.1 %while.28 = (s32[]{:T(128)}, f32[72,1024]{1,0:T(8,128)S(1)}, s32[]{:T(128)}, s32[]{:T(128)}, bf16[72,32768]{1,0:T(8,128)(2,1)}, /*index=5*/s32[32768]{0:T(1024)}...) while((s32[]{:T(128)}, f32[72,1024]{1,0:T(8,128)S(1)}, s32[]{:T(128)}, ...), condition=%wide.region_1.0_spmd, body=%wide.region_0.1_spmd.sunk | while | flops 304312320 | bytes 917675 | solution.py:69
  47.1 2.6 %fusion.42 = f32[72,1024]{1,0:T(8,128)S(1)} fusion(f32[72,1024]{1,0:T(8,128)S(1)} %get-tuple-element.430, s32[1024]{0:T(1024)S(1)} %get-tuple-element.446, s32[2048]{0:T(1024)S(1)} %dynamic_slice.31, bf16[72,32768]{1,0:T(8,128)(2,1)} %get-tuple-element.444, s32[]{:T(128)S(6)} %select_n.59, pred[2048]{0:T(1024)(128)(4,1)S(1)} %add_compare_fusion.2), kind=kOutput, calls=%fused_computation.6.clone.1 | convolution fusion | flops 304308224 | bytes 899076 | tf_op jit(solution)/shard_map/while/body/dot_general | solution.py:66
  51.1 2.6 %fusion.42 = f32[72,1024]{1,0:T(8,128)S(1)} fusion(f32[72,1024]{1,0:T(8,128)S(1)} %get-tuple-element.430, s32[1024]{0:T(1024)S(1)} %get-tuple-element.446, s32[2048]{0:T(1024)S(1)} %dynamic_slice.31, bf16[72,32768]{1,0:T(8,128)(2,1)} %get-tuple-element.444, s32[]{:T(128)S(6)} %select_n.59, pred[2048]{0:T(1024)(128)(4,1)S(1)} %add_compare_fusion.2), kind=kOutput, calls=%fused_computation.6.clone.1 | convolution fusion | flops 304308224 | bytes 899076 | tf_op jit(solution)/shard_map/while/body/dot_general | solution.py:66
  55.2 2.6 %fusion.42 = f32[72,1024]{1,0:T(8,128)S(1)} fusion(f32[72,1024]{1,0:T(8,128)S(1)} %get-tuple-element.430, s32[1024]{0:T(1024)S(1)} %get-tuple-element.446, s32[2048]{0:T(1024)S(1)} %dynamic_slice.31, bf16[72,32768]{1,0:T(8,128)(2,1)} %get-tuple-element.444, s32[]{:T(128)S(6)} %select_n.59, pred[2048]{0:T(1024)(128)(4,1)S(1)} %add_compare_fusion.2), kind=kOutput, calls=%fused_computation.6.clone.1 | convolution fusion | flops 304308224 | bytes 899076 | tf_op jit(solution)/shard_map/while/body/dot_general | solution.py:66
  59.2 2.6 %fusion.42 = f32[72,1024]{1,0:T(8,128)S(1)} fusion(f32[72,1024]{1,0:T(8,128)S(1)} %get-tuple-element.430, s32[1024]{0:T(1024)S(1)} %get-tuple-element.446, s32[2048]{0:T(1024)S(1)} %dynamic_slice.31, bf16[72,32768]{1,0:T(8,128)(2,1)} %get-tuple-element.444, s32[]{:T(128)S(6)} %select_n.59, pred[2048]{0:T(1024)(128)(4,1)S(1)} %add_compare_fusion.2), kind=kOutput, calls=%fused_computation.6.clone.1 | convolution fusion | flops 304308224 | bytes 899076 | tf_op jit(solution)/shard_map/while/body/dot_general | solution.py:66
  63.2 2.6 %fusion.42 = f32[72,1024]{1,0:T(8,128)S(1)} fusion(f32[72,1024]{1,0:T(8,128)S(1)} %get-tuple-element.430, s32[1024]{0:T(1024)S(1)} %get-tuple-element.446, s32[2048]{0:T(1024)S(1)} %dynamic_slice.31, bf16[72,32768]{1,0:T(8,128)(2,1)} %get-tuple-element.444, s32[]{:T(128)S(6)} %select_n.59, pred[2048]{0:T(1024)(128)(4,1)S(1)} %add_compare_fusion.2), kind=kOutput, calls=%fused_computation.6.clone.1 | convolution fusion | flops 304308224 | bytes 899076 | tf_op jit(solution)/shard_map/while/body/dot_general | solution.py:66
  67.2 2.6 %fusion.42 = f32[72,1024]{1,0:T(8,128)S(1)} fusion(f32[72,1024]{1,0:T(8,128)S(1)} %get-tuple-element.430, s32[1024]{0:T(1024)S(1)} %get-tuple-element.446, s32[2048]{0:T(1024)S(1)} %dynamic_slice.31, bf16[72,32768]{1,0:T(8,128)(2,1)} %get-tuple-element.444, s32[]{:T(128)S(6)} %select_n.59, pred[2048]{0:T(1024)(128)(4,1)S(1)} %add_compare_fusion.2), kind=kOutput, calls=%fused_computation.6.clone.1 | convolution fusion | flops 304308224 | bytes 899076 | tf_op jit(solution)/shard_map/while/body/dot_general | solution.py:66
  71.2 2.6 %fusion.42 = f32[72,1024]{1,0:T(8,128)S(1)} fusion(f32[72,1024]{1,0:T(8,128)S(1)} %get-tuple-element.430, s32[1024]{0:T(1024)S(1)} %get-tuple-element.446, s32[2048]{0:T(1024)S(1)} %dynamic_slice.31, bf16[72,32768]{1,0:T(8,128)(2,1)} %get-tuple-element.444, s32[]{:T(128)S(6)} %select_n.59, pred[2048]{0:T(1024)(128)(4,1)S(1)} %add_compare_fusion.2), kind=kOutput, calls=%fused_computation.6.clone.1 | convolution fusion | flops 304308224 | bytes 899076 | tf_op jit(solution)/shard_map/while/body/dot_general | solution.py:66
  75.2 2.6 %fusion.42 = f32[72,1024]{1,0:T(8,128)S(1)} fusion(f32[72,1024]{1,0:T(8,128)S(1)} %get-tuple-element.430, s32[1024]{0:T(1024)S(1)} %get-tuple-element.446, s32[2048]{0:T(1024)S(1)} %dynamic_slice.31, bf16[72,32768]{1,0:T(8,128)(2,1)} %get-tuple-element.444, s32[]{:T(128)S(6)} %select_n.59, pred[2048]{0:T(1024)(128)(4,1)S(1)} %add_compare_fusion.2), kind=kOutput, calls=%fused_computation.6.clone.1 | convolution fusion | flops 304308224 | bytes 899076 | tf_op jit(solution)/shard_map/while/body/dot_general | solution.py:66
  78.6 35.1 %all-to-all-start = ((f32[8,24,128]{2,1,0:T(8,128)}), f32[8,24,128]{2,1,0:T(8,128)S(1)}, u32[]{:S(2)}, u32[]{:S(2)}) async-start(f32[8,24,128]{2,1,0:T(8,128)} %copy.22), calls=%async_computation | async-start | bytes 196608 | tf_op jit(solution)/shard_map/all_to_all | solution.py:77
  114.8 4.1 %all-to-all-done = f32[8,24,128]{2,1,0:T(8,128)S(1)} async-done(((f32[8,24,128]{2,1,0:T(8,128)}), f32[8,24,128]{2,1,0:T(8,128)S(1)}, u32[]{:S(2)}, u32[]{:S(2)}) %all-to-all-start) | async-done | bytes 98336 | tf_op jit(solution)/shard_map/all_to_all | solution.py:77
  118.9 1.5 fusion.17
  121.2 22.9 %psum.14 = f32[24,500]{1,0:T(8,128)S(1)} all-reduce(f32[24,500]{1,0:T(8,128)S(1)} %fusion.20), channel_id=1, replica_groups=mesh['wide'=8,'narrow'=4] {'wide'}, use_global_device_ids=true, to_apply=%region_7.8 | all-reduce | flops 12000 | bytes 96000 | tf_op jit(solution)/shard_map/psum | solution.py:92
  144.4 12.0 %psum.15 = f32[2]{0:T(128)S(1)} all-reduce(f32[2]{0:T(128)S(1)} %reduce_sum.57), channel_id=1, replica_groups=mesh['wide'=8,'narrow'=4] {'narrow'}, use_global_device_ids=true, to_apply=%region_10.11 | all-reduce | flops 2 | bytes 16 | tf_op jit(solution)/shard_map/psum | solution.py:108
  (99 shorter events, 36.0 us)
Async XLA Ops:
  25.3 53.3 %all-to-all-start.1 = ((f32[8,1,128]{2,1,0:T(1,128)}), f32[8,1,128]{2,1,0:T(1,128)S(1)}, u32[]{:S(2)}, u32[]{:S(2)}) async-start(f32[8,1,128]{2,1,0:T(1,128)} %bitcast.3), calls=%async_computation.1 | async-start | bytes 8192 | tf_op jit(solution)/shard_map/all_to_all | solution.py:78
  78.6 40.3 %all-to-all-start = ((f32[8,24,128]{2,1,0:T(8,128)}), f32[8,24,128]{2,1,0:T(8,128)S(1)}, u32[]{:S(2)}, u32[]{:S(2)}) async-start(f32[8,24,128]{2,1,0:T(8,128)} %copy.22), calls=%async_computation | async-start | bytes 196608 | tf_op jit(solution)/shard_map/all_to_all | solution.py:77
where the time goes:
time: 161 us; the launch traced here: 159 us
  starting transfers between devices  40.3 us (25%)
  blocking collectives  34.8 us (22%)
  local copies, waits for them, and re-layouts  27.7 us (17%)
  matrix products  25.5 us (16%)
  other arithmetic  24.5 us (15%)
  waiting for transfers between devices  4.08 us (3%)
    all_to_all x1, starting transfers between devices, body(): lax.all_to_all(packed, 'wide', split_axis=0, concat_axis=0, tiled=True)  35.1 us
    psum x1, blocking collectives, body(): category_sums = lax.psum(category_part, 'wide')  22.9 us
    dot_general x8, matrix products, accumulate(): jnp.dot(values, member_table, preferred_element_type=jnp.float32)  21 us
    psum x1, blocking collectives, body(): grand_sum = lax.psum(kind_totals, 'narrow') / WEEKS  12 us
    reduce_sum x8, other arithmetic, lookup(): jnp.sum(jnp.where(own_columns[:, None] == block_slots[None, :], block_cat...  9.44 us
    unnamed x4, local copies, waits for them, and re-layouts  7.04 us
    dynamic_slice x8, local copies, waits for them, and re-layouts, accumulate(): target = lax.dynamic_slice_in_dim(sku_brand, offset, block_size, 0)  5.62 us
    dynamic_slice x8, local copies, waits for them, and re-layouts, lookup(): lax.dynamic_slice_in_dim(brand_category, offset, brand_block, 0)  5.54 us
  transfers between devices with their start and end apart: 2, of which 1 were waited for; matrix products, arithmetic and copies ran while one was open for 30% of the time, Pallas kernels for 0%

commit v1 on v0

--- a/solution.py
+++ b/solution.py
@@ -7,6 +7,11 @@
 WEEKS = 48
 CATS = 500
 CAP = 128
+
+
+def summed_here(array, mesh_axis):
+    shards = lax.all_gather(array, mesh_axis)
+    return jnp.sum(shards, axis=0)
 
 
 def body(measures, sku_brand, sku_count, brand_slot, brand_category):
@@ -89,7 +94,7 @@
     category_part = jnp.dot(
         owned_sums, membership, precision=lax.Precision.HIGHEST, preferred_element_type=jnp.float32
     )
-    category_sums = lax.psum(category_part, "wide")
+    category_sums = summed_here(category_part, "wide")
     brand_category_sum = jnp.dot(
         category_sums,
         membership.T,

time: 161 us -> 147 us (0.913)
  blocking collectives: 34.8 us -> 20.7 us
    psum x1 -> x0, blocking collectives: 22.9 us -> none  [body(): category_sums = lax.psum(category_part, 'wide')]
    all_gather x0 -> x1, blocking collectives: none -> 8.71 us  [summed_here(): shards = lax.all_gather(array, mesh_axis)]
  transfers between devices with their start and end apart: 2 -> 2, of which waited for: 1 -> 1; matrix products, arithmetic and copies ran while one was open for 30% -> 33% of each run, Pallas kernels for 0% -> 0%
where the time goes in v1:
time: 147 us; the launch traced here: 145 us
  starting transfers between devices  40.3 us (27%)
  local copies, waits for them, and re-layouts  27.8 us (19%)
  matrix products  25.5 us (17%)
  other arithmetic  24.5 us (17%)
  blocking collectives  20.7 us (14%)
  waiting for transfers between devices  4.08 us (3%)
    all_to_all x1, starting transfers between devices, body(): lax.all_to_all(packed, 'wide', split_axis=0, concat_axis=0, tiled=True)  35.1 us
    dot_general x8, matrix products, accumulate(): jnp.dot(values, member_table, preferred_element_type=jnp.float32)  21 us
    psum x1, blocking collectives, body(): grand_sum = lax.psum(kind_totals, 'narrow') / WEEKS  12 us
    reduce_sum x8, other arithmetic, lookup(): jnp.sum(jnp.where(own_columns[:, None] == block_slots[None, :], block_cat...  9.44 us
    all_gather x1, blocking collectives, summed_here(): shards = lax.all_gather(array, mesh_axis)  8.71 us
    unnamed x4, local copies, waits for them, and re-layouts  7.04 us
    dynamic_slice x8, local copies, waits for them, and re-layouts, accumulate(): target = lax.dynamic_slice_in_dim(sku_brand, offset, block_size, 0)  5.62 us
    dynamic_slice x8, local copies, waits for them, and re-layouts, lookup(): lax.dynamic_slice_in_dim(brand_category, offset, brand_block, 0)  5.54 us
  transfers between devices with their start and end apart: 2, of which 1 were waited for; matrix products, arithmetic and copies ran while one was open for 33% of the time, Pallas kernels for 0%

profile of v1, /device:TPU:0, one launch (start us, length us, event | category | flops | bytes accessed | tf_op | source)
XLA Modules:
  0.0 145.0 jit_solution(16472053813028527784)
XLA Ops:
  1.4 23.3 %while.29 = (s32[]{:T(128)}, s32[1024]{0:T(1024)S(1)}, s32[1024]{0:T(1024)S(1)}, f32[500]{0:T(512)S(1)}, s32[1024]{0:T(1024)S(1)}, /*index=5*/s32[8192]{0:T(1024...) while((s32[]{:T(128)}, s32[1024]{0:T(1024)S(1)}, ...), condition=%wide.region_6.7_spmd.clone, body=%wide.region_2.6_spmd.clone.sunk | while | flops 7832059 | bytes 90110 | solution.py:55
  2.7 1.2 select_reduce_fusion.3
  5.7 1.2 select_reduce_fusion.3
  17.3 1.2 select_reduce_fusion.3
  20.2 1.2 select_reduce_fusion.3
  25.3 5.2 %all-to-all-start.1 = ((f32[8,1,128]{2,1,0:T(1,128)}), f32[8,1,128]{2,1,0:T(1,128)S(1)}, u32[]{:S(2)}, u32[]{:S(2)}) async-start(f32[8,1,128]{2,1,0:T(1,128)} %bitcast.3), calls=%async_computation.1 | async-start | bytes 8192 | tf_op jit(solution)/shard_map/all_to_all | solution.py:83
  31.1 5.6 %copy.20 = f32[2,12,32768]{2,1,0:T(8,128)} copy(f32[2,12,32768]{2,0,1:T(2,128)} %param.9) | data formatting | bytes 6291456 | tf_op args[0]
  36.8 2.6 %reshape.62 = f32[24,32768]{1,0:T(8,128)S(1)} reshape(f32[2,12,32768]{2,1,0:T(8,128)} %copy.20) | data formatting | bytes 6291456 | tf_op jit(solution)/shard_map/reshape | solution.py:20
  39.3 2.5 %fusion.31 = (bf16[24,32768]{1,0:T(8,128)(2,1)}, bf16[24,32768]{1,0:T(8,128)(2,1)}, bf16[24,32768]{1,0:T(8,128)(2,1)}) fusion(f32[24,32768]{1,0:T(8,128)S(1)} %reshape.62), kind=kLoop, calls=%fused_computation.49 | loop fusion | flops 5505024 | bytes 7864320 | tf_op jit(solution)/shard_map/convert_element_type | solution.py:56
  41.8 3.9 %pad_maximum_fusion = bf16[72,32768]{1,0:T(8,128)(2,1)} fusion(bf16[24,32768]{1,0:T(8,128)(2,1)} %get-tuple-element.277, bf16[24,32768]{1,0:T(8,128)(2,1)} %get-tuple-element.278, bf16[24,32768]{1,0:T(8,128)(2,1)} %get-tuple-element.276), kind=kLoop, calls=%fused_computation.23 | loop fusion | flops 14155776 | bytes 9437184 | tf_op jit(solution)/shard_map/concatenate | solution.py:60
  45.7 32.1 %while.28 = (s32[]{:T(128)}, f32[72,1024]{1,0:T(8,128)S(1)}, s32[]{:T(128)}, s32[]{:T(128)}, bf16[72,32768]{1,0:T(8,128)(2,1)}, /*index=5*/s32[32768]{0:T(1024)}...) while((s32[]{:T(128)}, f32[72,1024]{1,0:T(8,128)S(1)}, s32[]{:T(128)}, ...), condition=%wide.region_1.0_spmd, body=%wide.region_0.1_spmd.sunk | while | flops 304312320 | bytes 917675 | solution.py:74
  47.1 2.6 %fusion.41 = f32[72,1024]{1,0:T(8,128)S(1)} fusion(f32[72,1024]{1,0:T(8,128)S(1)} %get-tuple-element.428, s32[1024]{0:T(1024)S(1)} %get-tuple-element.444, s32[2048]{0:T(1024)S(1)} %dynamic_slice.31, bf16[72,32768]{1,0:T(8,128)(2,1)} %get-tuple-element.442, s32[]{:T(128)S(6)} %select_n.59, pred[2048]{0:T(1024)(128)(4,1)S(1)} %add_compare_fusion.2), kind=kOutput, calls=%fused_computation.6.clone.1 | convolution fusion | flops 304308224 | bytes 899076 | tf_op jit(solution)/shard_map/while/body/dot_general | solution.py:71
  51.1 2.6 %fusion.41 = f32[72,1024]{1,0:T(8,128)S(1)} fusion(f32[72,1024]{1,0:T(8,128)S(1)} %get-tuple-element.428, s32[1024]{0:T(1024)S(1)} %get-tuple-element.444, s32[2048]{0:T(1024)S(1)} %dynamic_slice.31, bf16[72,32768]{1,0:T(8,128)(2,1)} %get-tuple-element.442, s32[]{:T(128)S(6)} %select_n.59, pred[2048]{0:T(1024)(128)(4,1)S(1)} %add_compare_fusion.2), kind=kOutput, calls=%fused_computation.6.clone.1 | convolution fusion | flops 304308224 | bytes 899076 | tf_op jit(solution)/shard_map/while/body/dot_general | solution.py:71
  55.2 2.6 %fusion.41 = f32[72,1024]{1,0:T(8,128)S(1)} fusion(f32[72,1024]{1,0:T(8,128)S(1)} %get-tuple-element.428, s32[1024]{0:T(1024)S(1)} %get-tuple-element.444, s32[2048]{0:T(1024)S(1)} %dynamic_slice.31, bf16[72,32768]{1,0:T(8,128)(2,1)} %get-tuple-element.442, s32[]{:T(128)S(6)} %select_n.59, pred[2048]{0:T(1024)(128)(4,1)S(1)} %add_compare_fusion.2), kind=kOutput, calls=%fused_computation.6.clone.1 | convolution fusion | flops 304308224 | bytes 899076 | tf_op jit(solution)/shard_map/while/body/dot_general | solution.py:71
  59.2 2.6 %fusion.41 = f32[72,1024]{1,0:T(8,128)S(1)} fusion(f32[72,1024]{1,0:T(8,128)S(1)} %get-tuple-element.428, s32[1024]{0:T(1024)S(1)} %get-tuple-element.444, s32[2048]{0:T(1024)S(1)} %dynamic_slice.31, bf16[72,32768]{1,0:T(8,128)(2,1)} %get-tuple-element.442, s32[]{:T(128)S(6)} %select_n.59, pred[2048]{0:T(1024)(128)(4,1)S(1)} %add_compare_fusion.2), kind=kOutput, calls=%fused_computation.6.clone.1 | convolution fusion | flops 304308224 | bytes 899076 | tf_op jit(solution)/shard_map/while/body/dot_general | solution.py:71
  63.2 2.6 %fusion.41 = f32[72,1024]{1,0:T(8,128)S(1)} fusion(f32[72,1024]{1,0:T(8,128)S(1)} %get-tuple-element.428, s32[1024]{0:T(1024)S(1)} %get-tuple-element.444, s32[2048]{0:T(1024)S(1)} %dynamic_slice.31, bf16[72,32768]{1,0:T(8,128)(2,1)} %get-tuple-element.442, s32[]{:T(128)S(6)} %select_n.59, pred[2048]{0:T(1024)(128)(4,1)S(1)} %add_compare_fusion.2), kind=kOutput, calls=%fused_computation.6.clone.1 | convolution fusion | flops 304308224 | bytes 899076 | tf_op jit(solution)/shard_map/while/body/dot_general | solution.py:71
  67.2 2.6 %fusion.41 = f32[72,1024]{1,0:T(8,128)S(1)} fusion(f32[72,1024]{1,0:T(8,128)S(1)} %get-tuple-element.428, s32[1024]{0:T(1024)S(1)} %get-tuple-element.444, s32[2048]{0:T(1024)S(1)} %dynamic_slice.31, bf16[72,32768]{1,0:T(8,128)(2,1)} %get-tuple-element.442, s32[]{:T(128)S(6)} %select_n.59, pred[2048]{0:T(1024)(128)(4,1)S(1)} %add_compare_fusion.2), kind=kOutput, calls=%fused_computation.6.clone.1 | convolution fusion | flops 304308224 | bytes 899076 | tf_op jit(solution)/shard_map/while/body/dot_general | solution.py:71
  71.2 2.6 %fusion.41 = f32[72,1024]{1,0:T(8,128)S(1)} fusion(f32[72,1024]{1,0:T(8,128)S(1)} %get-tuple-element.428, s32[1024]{0:T(1024)S(1)} %get-tuple-element.444, s32[2048]{0:T(1024)S(1)} %dynamic_slice.31, bf16[72,32768]{1,0:T(8,128)(2,1)} %get-tuple-element.442, s32[]{:T(128)S(6)} %select_n.59, pred[2048]{0:T(1024)(128)(4,1)S(1)} %add_compare_fusion.2), kind=kOutput, calls=%fused_computation.6.clone.1 | convolution fusion | flops 304308224 | bytes 899076 | tf_op jit(solution)/shard_map/while/body/dot_general | solution.py:71
  75.2 2.6 %fusion.41 = f32[72,1024]{1,0:T(8,128)S(1)} fusion(f32[72,1024]{1,0:T(8,128)S(1)} %get-tuple-element.428, s32[1024]{0:T(1024)S(1)} %get-tuple-element.444, s32[2048]{0:T(1024)S(1)} %dynamic_slice.31, bf16[72,32768]{1,0:T(8,128)(2,1)} %get-tuple-element.442, s32[]{:T(128)S(6)} %select_n.59, pred[2048]{0:T(1024)(128)(4,1)S(1)} %add_compare_fusion.2), kind=kOutput, calls=%fused_computation.6.clone.1 | convolution fusion | flops 304308224 | bytes 899076 | tf_op jit(solution)/shard_map/while/body/dot_general | solution.py:71
  78.6 35.1 %all-to-all-start = ((f32[8,24,128]{2,1,0:T(8,128)}), f32[8,24,128]{2,1,0:T(8,128)S(1)}, u32[]{:S(2)}, u32[]{:S(2)}) async-start(f32[8,24,128]{2,1,0:T(8,128)} %copy.21), calls=%async_computation | async-start | bytes 196608 | tf_op jit(solution)/shard_map/all_to_all | solution.py:82
  114.8 4.1 %all-to-all-done = f32[8,24,128]{2,1,0:T(8,128)S(1)} async-done(((f32[8,24,128]{2,1,0:T(8,128)}), f32[8,24,128]{2,1,0:T(8,128)S(1)}, u32[]{:S(2)}, u32[]{:S(2)}) %all-to-all-start) | async-done | bytes 98336 | tf_op jit(solution)/shard_map/all_to_all | solution.py:82
  118.9 1.5 %fusion.17 = f32[24,1024]{1,0:T(8,128)S(1)} fusion(s32[1024]{0:T(1024)S(1)} %bitcast.26, f32[8,24,128]{2,1,0:T(8,128)S(1)} %all-to-all-done), kind=kOutput, calls=%fused_computation.25 | convolution fusion | flops 303038464 | bytes 200704 | tf_op jit(solution)/shard_map/dot_general | solution.py:90
  121.2 8.7 %all-gather = f32[192,500]{1,0:T(8,128)S(1)} all-gather(f32[24,500]{1,0:T(8,128)S(1)} %fusion.20), channel_id=2, replica_groups=mesh['wide'=8,'narrow'=4] {'wide'}, dimensions={0}, use_global_device_ids=true | all-gather | bytes 432000 | tf_op jit(solution)/shard_map/all_gather | solution.py:13
  130.4 12.0 %psum.7 = f32[2]{0:T(128)S(1)} all-reduce(f32[2]{0:T(128)S(1)} %reduce_sum.67), channel_id=1, replica_groups=mesh['wide'=8,'narrow'=4] {'narrow'}, use_global_device_ids=true, to_apply=%region_10.11 | all-reduce | flops 2 | bytes 16 | tf_op jit(solution)/shard_map/psum | solution.py:113
  (103 shorter events, 36.1 us)
Async XLA Ops:
  25.3 53.3 %all-to-all-start.1 = ((f32[8,1,128]{2,1,0:T(1,128)}), f32[8,1,128]{2,1,0:T(1,128)S(1)}, u32[]{:S(2)}, u32[]{:S(2)}) async-start(f32[8,1,128]{2,1,0:T(1,128)} %bitcast.3), calls=%async_computation.1 | async-start | bytes 8192 | tf_op jit(solution)/shard_map/all_to_all | solution.py:83
  78.6 40.3 %all-to-all-start = ((f32[8,24,128]{2,1,0:T(8,128)}), f32[8,24,128]{2,1,0:T(8,128)S(1)}, u32[]{:S(2)}, u32[]{:S(2)}) async-start(f32[8,24,128]{2,1,0:T(8,128)} %copy.21), calls=%async_computation | async-start | bytes 196608 | tf_op jit(solution)/shard_map/all_to_all | solution.py:82
